TPU v7x, 32 devices: a whole 2x2x4 slice. The times are simulated.
32 devices in a mesh: dp: 2 (over y), row: 4 (over x, core), col: 4 (over z).
Axes of the slice: x: 2, y: 2, z: 4, core: 2. Of those that a mesh axis runs over, the one named last changes fastest.
Arguments:
- tokens: bfloat16 [2048, 8192], P(('dp', 'col'), 'row'), may hold values from -6 to 6
- frozen_weight: bfloat16 [8192, 8192], P('row', 'col'), may hold values from -0.0625 to 0.0625
- input_adapter_factor: bfloat16 [16, 8192], P(None, 'row'), may hold values from -0.0625 to 0.0625
- output_adapter_factor: bfloat16 [16, 8192], P(None, 'col'), may hold values from -1.5 to 1.5
- magnitude: float32 [8192], P('col'), may hold values from 0.5 to 2
- cotangent: bfloat16 [2048, 8192], P(('dp', 'row'), 'col'), may hold values from -6 to 6
- sequence_lengths: int32 [2, 8], P('dp'), may hold values from 1 to 512, 1024 in all within a row
Outputs:
- projected: bfloat16 [2048, 8192], P(('dp', 'row'), 'col')
- grad_mag: float32 [8192], P('col')
- input_factor_gradient: float32 [16, 8192], P(None, 'row')
- grad_b: float32 [16, 8192], P(None, 'col')
Inputs may be any that keep to these rules, and one draw needn't show every extreme that they name: `sequence_lengths`: each group's 8 lengths sum to 1024, and one of them is exactly 512.
All inputs are finite; a program needn't handle non-finite values.
Results may differ from a plain program's by a relative error of at most 0.0052.
Values may be sent and summed in bfloat16 or wider, within the bound.
No kernel may reach another device: no remote copies, remote signals or barrier semaphores. Data moves between devices by JAX's collectives and lax.ppermute only.
A program may use at most 64 MiB of HBM per device.

v0:
```python
import jax
import jax.numpy as jnp
from jax import lax
from jax.sharding import PartitionSpec as P

norm_eps = 1e-06
highest_precision = lax.Precision.HIGHEST


def contract_product(left, right, left_dim, right_dim):
    return lax.dot_general(
        left, right, (((left_dim,), (right_dim,)), ((), ())), preferred_element_type=jnp.float32
    )


def per_device(
    tokens,
    frozen_weight,
    input_adapter_factor,
    output_adapter_factor,
    magnitude,
    cotangent,
    sequence_lengths,
):
    row_count = lax.axis_size("row")
    col_count = lax.axis_size("col")
    row_index = lax.axis_index("row")
    col_index = lax.axis_index("col")
    group_index = lax.axis_index("dp")
    local_rows = tokens.shape[0]
    group_rows = local_rows * col_count
    block_rows = group_rows // row_count
    adapter_rank_size = input_adapter_factor.shape[0]
    low_rank_update = contract_product(input_adapter_factor, output_adapter_factor, 0, 0)
    merged = frozen_weight.astype(jnp.float32) + low_rank_update
    norm_terms = jnp.sum(merged * merged, axis=0)
    gram_partial_terms = contract_product(input_adapter_factor, input_adapter_factor, 1, 1)
    merged_factor_terms = jnp.dot(
        input_adapter_factor, frozen_weight, preferred_element_type=jnp.float32
    ) + jnp.dot(
        gram_partial_terms, output_adapter_factor.astype(jnp.float32), precision=highest_precision
    )
    portion = lax.all_gather(tokens, "col", axis=0, tiled=True)
    base_piece = jnp.dot(portion, frozen_weight, preferred_element_type=jnp.float32)
    down_portion = contract_product(portion, input_adapter_factor, 1, 1)
    frozen_rows, down_rows = (
        lax.psum_scatter(base_piece, "row", scatter_dimension=0, tiled=True),
        lax.psum_scatter(down_portion, "row", scatter_dimension=0, tiled=True),
    )
    norm_sq, merged_input_factor = lax.psum((norm_terms, merged_factor_terms), "row")
    down_activations = down_rows.astype(jnp.bfloat16)
    col_norm = jnp.sqrt(norm_sq + norm_eps)
    col_scale = magnitude / col_norm
    query_projection = frozen_rows + jnp.dot(
        down_activations, output_adapter_factor, preferred_element_type=jnp.float32
    )
    projected = (query_projection * col_scale[None, :]).astype(jnp.bfloat16)
    lengths = sequence_lengths[0]
    ends = jnp.cumsum(lengths, dtype=jnp.int32)
    starts = ends - lengths
    positions = row_index * block_rows + jnp.arange(block_rows, dtype=jnp.int32)
    inside = (positions[:, None] >= starts[None, :]) & (positions[:, None] < ends[None, :])
    inverse = 1.0 / lengths.astype(jnp.float32)
    weights = jnp.sum(jnp.where(inside, inverse[None, :], jnp.float32(0.0)), axis=1)
    grad_out = cotangent.astype(jnp.float32) * weights[:, None]
    scale_terms = jnp.sum(grad_out * query_projection, axis=0)
    projection_gradient = (grad_out * col_scale[None, :]).astype(jnp.bfloat16)
    bgrad_terms = contract_product(down_activations, projection_gradient, 0, 0)
    scale_grad, bgrad_data = lax.psum((scale_terms, bgrad_terms), ("dp", "row"))
    grad_mag = scale_grad / col_norm
    norm_coefficient = -scale_grad * magnitude / (col_norm * col_norm * col_norm)
    grad_b = bgrad_data + merged_input_factor * norm_coefficient[None, :]
    backward_terms = contract_product(projection_gradient, output_adapter_factor, 1, 1)
    padded = lax.dynamic_update_slice_in_dim(
        jnp.zeros((group_rows, adapter_rank_size), jnp.float32),
        backward_terms,
        row_index * block_rows,
        0,
    )
    backward_rows = lax.psum(padded, ("row", "col")).astype(jnp.bfloat16)
    back_mine = lax.dynamic_slice_in_dim(backward_rows, col_index * local_rows, local_rows, 0)
    row_term = contract_product(back_mine, tokens, 0, 0)
    scaled_output_factor = (
        output_adapter_factor.astype(jnp.float32) * norm_coefficient[None, :]
    ).astype(jnp.bfloat16)
    norm_term = contract_product(scaled_output_factor, frozen_weight, 1, 1) + jnp.dot(
        contract_product(scaled_output_factor, output_adapter_factor, 1, 1),
        input_adapter_factor.astype(jnp.float32),
        precision=highest_precision,
    )
    first_group = (group_index == 0).astype(jnp.float32)
    input_factor_gradient = lax.psum(row_term + first_group * norm_term, ("dp", "col"))
    return (projected, grad_mag, input_factor_gradient, grad_b)


def solution(mesh):
    in_specs = (
        P(("dp", "col"), "row"),
        P("row", "col"),
        P(None, "row"),
        P(None, "col"),
        P("col"),
        P(("dp", "row"), "col"),
        P("dp", None),
    )
    out_specs = (P(("dp", "row"), "col"), P("col"), P(None, "row"), P(None, "col"))
    return jax.shard_map(
        per_device, mesh=mesh, in_specs=in_specs, out_specs=out_specs, check_vma=False
    )
```

profile of v0, /device:TPU:0, one launch (start us, length us, event | category | flops | bytes accessed | tf_op | source)
XLA Modules:
  0.0 366.2 jit_solution(13270679273868545477)
XLA Ops:
  7.2 0.0 all-gather.2.cloned.1.call-start
  7.2 0.7 all-gather.2.cloned.1.call-update
  7.9 0.0 reduce-scatter.5.cloned.1.call-start
  8.0 85.1 %all-gather.2.cloned.1.call-done = bf16[1024,2048]{1,0:T(8,128)(2,1)} async-done(((bf16[256,2048]{1,0:T(8,128)(2,1)}), bf16[1024,2048]{1,0:T(8,128)(2,1)}) %all-gather.2.cloned.1.call-update) | async-done | bytes 4194320 | tf_op jit(solution)/shard_map/all_gather | solution.py:43
  93.1 4.0 %fusion.14 = f32[1024,16]{0,1:T(8,128)} fusion(bf16[1024,2048]{1,0:T(8,128)(2,1)} %all-gather.2.cloned.1.call-done, bf16[16,2048]{1,0:T(8,128)(2,1)S(1)} %copy-done), kind=kOutput, calls=%fused_computation.33 | convolution fusion | flops 67108864 | bytes 4325376 | tf_op jit(solution)/shard_map/dot_general | solution.py:11
  97.1 0.0 reduce-scatter.3.cloned.1.call-start
  97.1 14.4 %fusion.13 = f32[1024,2048]{1,0:T(8,128)} fusion(bf16[1024,2048]{1,0:T(8,128)(2,1)} %all-gather.2.cloned.1.call-done, bf16[2048,2048]{1,0:T(8,128)(2,1)} %param.8), kind=kOutput, calls=%fused_computation.32 | convolution fusion | flops 8589934592 | bytes 20971520 | tf_op jit(solution)/shard_map/dot_general | solution.py:44
  111.6 0.0 all-reduce.8.cloned.1.call-start
  111.6 0.1 fusion.16
  111.8 4.6 %fusion.15 = f32[16,2048]{1,0:T(8,128)S(1)} fusion(bf16[16,2048]{1,0:T(8,128)(2,1)S(1)} %copy-done, bf16[2048,2048]{1,0:T(8,128)(2,1)} %param.8), kind=kOutput, calls=%fused_computation.34 | convolution fusion | flops 134217728 | bytes 8585216 | tf_op jit(solution)/shard_map/dot_general | solution.py:38
  116.4 0.9 convolution_add_fusion.1
  117.3 0.0 all-reduce.6.cloned.1.call-start
  117.4 5.9 %multiply_reduce_fusion = f32[2048]{0:T(1024)S(1)} fusion(bf16[2048,2048]{1,0:T(8,128)(2,1)} %param.8, bf16[16,2048]{1,0:T(8,128)(2,1)S(1)} %copy-done, bf16[16,2048]{1,0:T(8,128)(2,1)S(1)} %copy-done.2), kind=kOutput, calls=%fused_computation | convolution fusion | flops 150992896 | bytes 8527872 | tf_op jit(solution)/shard_map/dot_general | solution.py:11
  123.3 0.2 reduce-window.4
  123.5 6.5 %psum.42 = f32[2048]{0:T(1024)S(1)} all-reduce(f32[2048]{0:T(1024)S(1)} %multiply_reduce_fusion), channel_id=1, replica_groups=mesh['dp'=2,'row'=4,'col'=4] {'row'}, use_global_device_ids=true, to_apply=%region_3.0 | all-reduce | flops 2048 | bytes 16384 | tf_op jit(solution)/shard_map/psum | solution.py:50
  130.1 0.1 select_reduce_fusion
  130.2 0.5 convolution_dynamic-update-slice_fusion
  130.7 69.2 %psum.44 = bf16[1024,16]{1,0:T(8,128)(2,1)S(1)} all-reduce(f32[1024,16]{1,0:T(8,128)S(1)} %convolution_dynamic-update-slice_fusion), channel_id=1, replica_groups=mesh['dp'=2,'row'=4,'col'=4] {'row','col'}, use_global_device_ids=true, to_apply=%region_8.9 | all-reduce | flops 16384 | bytes 98304 | tf_op jit(solution)/shard_map/psum | solution.py:80
  200.0 1.8 fusion.1
  201.8 0.0 all-reduce.4.cloned.1.call-start
  201.9 3.2 multiply_reduce_fusion.1
  205.1 12.1 %psum.43 = f32[2048]{0:T(1024)S(1)} all-reduce(f32[2048]{0:T(1024)S(1)} %get-tuple-element.4), channel_id=1, replica_groups=mesh['dp'=2,'row'=4,'col'=4] {'dp','row'}, use_global_device_ids=true, to_apply=%region_7.8 | all-reduce | flops 2048 | bytes 16384 | tf_op jit(solution)/shard_map/psum | solution.py:69
  217.1 0.6 fusion.6
  217.8 5.7 %fusion.3 = f32[16,2048]{1,0:T(8,128)S(1)} fusion(bf16[2048,2048]{1,0:T(8,128)(2,1)} %param.8, bf16[16,2048]{1,0:T(8,128)(2,1)S(1)} %copy-done.2, f32[2048]{0:T(1024)S(1)} %get-tuple-element.6), kind=kOutput, calls=%fused_computation.16 | convolution fusion | flops 134316032 | bytes 8593408 | tf_op jit(solution)/shard_map/dot_general | solution.py:11
  223.5 0.1 fusion.2
  223.6 0.2 fusion
  223.9 0.9 convolution_add_fusion.3
  224.8 2.4 all-reduce.8.cloned.1.call-done
  227.2 57.0 %all-reduce.6.cloned.1.call-done = f32[16,2048]{1,0:T(8,128)} async-done(((f32[16,2048]{1,0:T(8,128)}), f32[16,2048]{1,0:T(8,128)}) %all-reduce.6.cloned.1.call-update) | async-done | bytes 131088 | tf_op jit(solution)/shard_map/psum | solution.py:69
  284.2 1.6 multiply_add_fusion
  285.9 71.9 %all-reduce.4.cloned.1.call-done = f32[16,2048]{1,0:T(8,128)} async-done(((f32[16,2048]{1,0:T(8,128)}), f32[16,2048]{1,0:T(8,128)}) %all-reduce.4.cloned.1.call-update) | async-done | bytes 131088 | tf_op jit(solution)/shard_map/psum | solution.py:92
  357.8 1.6 copy.15
  (24 shorter events, 0.2 us)
Async XLA Ops:
  7.2 85.9 %copy-start = (bf16[16,2048]{1,0:T(8,128)(2,1)S(1)}, bf16[16,2048]{1,0:T(8,128)(2,1)}, u32[]{:S(2)}) copy-start(bf16[16,2048]{1,0:T(8,128)(2,1)} %param.9) | copy-start | bytes 196612
  7.2 85.9 %all-gather.2.cloned.1.call-start = ((), (), s32[]{:S(2)}) async-start(), calls=%async_computation.2 | async-start | bytes 5242880 | tf_op jit(solution)/shard_map/all_gather | solution.py:43
  7.9 192.0 %reduce-scatter.5.cloned.1.call-start = ((), (), s32[]{:S(2)}) async-start(), calls=%async_computation.4 | async-start | bytes 81920 | tf_op jit(solution)/shard_map/reduce_scatter | solution.py:48
  97.1 104.8 %reduce-scatter.3.cloned.1.call-start = ((), (), s32[]{:S(2)}) async-start(), calls=%async_computation.3 | async-start | bytes 10485760 | tf_op jit(solution)/shard_map/reduce_scatter | solution.py:47
  111.6 115.7 %all-reduce.8.cloned.1.call-start = ((), (), s32[]{:S(2)}) async-start(), calls=%async_computation.7 | async-start | bytes 262144 | tf_op jit(solution)/shard_map/psum | solution.py:50
  111.8 4.6 %copy-start.2 = (bf16[16,2048]{1,0:T(8,128)(2,1)S(1)}, bf16[16,2048]{1,0:T(8,128)(2,1)}, u32[]{:S(2)}) copy-start(bf16[16,2048]{1,0:T(8,128)(2,1)} %param.10) | copy-start | bytes 196612
  117.3 166.9 %all-reduce.6.cloned.1.call-start = ((), (), s32[]{:S(2)}) async-start(), calls=%async_computation.6 | async-start | bytes 262144 | tf_op jit(solution)/shard_map/psum | solution.py:69
  117.3 5.9 %copy-start.5 = (s32[1,8]{1,0:T(1,128)S(1)}, s32[1,8]{1,0:T(1,128)}, u32[]{:S(2)}) copy-start(s32[1,8]{1,0:T(1,128)} %param.13) | copy-start | bytes 100
  117.4 12.7 %copy-start.4 = (f32[2048]{0:T(1024)S(1)}, f32[2048]{0:T(1024)}, u32[]{:S(2)}) copy-start(f32[2048]{0:T(1024)} %param.11) | copy-start | bytes 24580
  117.4 12.8 %copy-start.3 = (bf16[256,2048]{1,0:T(8,128)(2,1)S(1)}, bf16[256,2048]{1,0:T(8,128)(2,1)}, u32[]{:S(2)}) copy-start(bf16[256,2048]{1,0:T(8,128)(2,1)} %param.12) | copy-start | bytes 3145732
  201.8 156.0 %all-reduce.4.cloned.1.call-start = ((), (), s32[]{:S(2)}) async-start(), calls=%async_computation.5 | async-start | bytes 262144 | tf_op jit(solution)/shard_map/psum | solution.py:92
  217.8 6.1 %copy-start.1 = (bf16[256,2048]{1,0:T(8,128)(2,1)S(1)}, bf16[256,2048]{1,0:T(8,128)(2,1)}, u32[]{:S(2)}) copy-start(bf16[256,2048]{1,0:T(8,128)(2,1)} %param.7) | copy-start | bytes 3145732
Sparse Core Ops, SparseCore 0:
  9.6 83.4 all-gather.1
  97.2 18.0 reduce-scatter.4
  117.9 75.6 reduce-scatter.2
  195.8 31.4 all-reduce.7
  230.7 53.4 all-reduce.5
  288.0 69.7 all-reduce.3
where the time goes:
time: 367 us; the launch traced here: 366 us
  waiting for transfers between devices  217 us (59%)
  blocking collectives  87.8 us (24%)
  matrix products  42.5 us (12%)
  between operations  14.3 us (4%)
    all_gather x1, waiting for transfers between devices, per_device(): portion = lax.all_gather(tokens, 'col', axis=0, tiled=True)  85.1 us
    psum x1, waiting for transfers between devices, per_device(): lax.psum(row_term + first_group * norm_term, ('dp', 'col'))  71.9 us
    psum x1, blocking collectives, per_device(): backward_rows = lax.psum(padded, ('row', 'col')).astype(jnp.bfloat16)  69.2 us
    psum x1, waiting for transfers between devices, per_device(): scale_grad, bgrad_data = lax.psum((scale_terms, bgrad_terms), ('dp', 'row'))  57 us
    dot_general x8, matrix products, contract_product(): lax.dot_general(left, right, (((left_dim,), (right_dim,)), ((), ())), pre...  19.1 us
    dot_general x1, matrix products, per_device(): jnp.dot(portion, frozen_weight, preferred_element_type=jnp.float32)  14.4 us
    psum x1, blocking collectives, per_device(): scale_grad, bgrad_data = lax.psum((scale_terms, bgrad_terms), ('dp', 'row'))  12.1 us
  transfers between devices with their start and end apart: 6, of which 4 were waited for; matrix products, arithmetic and copies ran while one was open for 11% of the time, Pallas kernels for 0%

commit v1 on v0

--- a/solution.py
+++ b/solution.py
@@ -40,7 +40,12 @@
     ) + jnp.dot(
         gram_partial_terms, output_adapter_factor.astype(jnp.float32), precision=highest_precision
     )
-    portion = lax.all_gather(tokens, "col", axis=0, tiled=True)
+    ring = [tokens]
+    for hop in range(3):
+        ring.append(lax.ppermute(ring[-1], "col", [(dev, (dev + 1) % 4) for dev in range(4)]))
+    portion = jnp.roll(
+        jnp.concatenate(ring[::-1], axis=0), (lax.axis_index("col") + 1) * ring[0].shape[0], axis=0
+    )
     base_piece = jnp.dot(portion, frozen_weight, preferred_element_type=jnp.float32)
     down_portion = contract_product(portion, input_adapter_factor, 1, 1)
     frozen_rows, down_rows = (

time: 367 us -> 366 us (level)
  waiting for transfers between devices: 217 us -> 207 us
  local copies, waits for them, and re-layouts: 1.64 us -> 9.21 us
  other arithmetic: 2.55 us -> 7.32 us
  matrix products: 42.5 us -> 38.1 us
    all_gather x1 -> x0, waiting for transfers between devices: 85.1 us -> none  [per_device(): portion = lax.all_gather(tokens, 'col', axis=0, tiled=True)]
    ppermute x0 -> x3, waiting for transfers between devices: none -> 76.9 us  [per_device(): lax.ppermute(ring[-1], 'col', [(dev, (dev + 1) % 4) for dev in range(4)])]
    unnamed x13 -> x24, local copies, waits for them, and re-layouts: 1.6 us -> 9.11 us
    reduce_sum x0 -> x1, other arithmetic: none -> 4.07 us  [per_device(): scale_terms = jnp.sum(grad_out * query_projection, axis=0)]
  transfers between devices with their start and end apart: 6 -> 8, of which waited for: 4 -> 6; matrix products, arithmetic and copies ran while one was open for 11% -> 12% of each run, Pallas kernels for 0% -> 0%
where the time goes in v1:
time: 366 us; the launch traced here: 365 us
  waiting for transfers between devices  207 us (57%)
  blocking collectives  86.4 us (24%)
  matrix products  38.1 us (10%)
  between operations  14 us (4%)
  local copies, waits for them, and re-layouts  9.21 us (3%)
  other arithmetic  7.32 us (2%)
    ppermute x3, waiting for transfers between devices, per_device(): lax.ppermute(ring[-1], 'col', [(dev, (dev + 1) % 4) for dev in range(4)])  76.9 us
    psum x1, waiting for transfers between devices, per_device(): lax.psum(row_term + first_group * norm_term, ('dp', 'col'))  71.9 us
    psum x1, blocking collectives, per_device(): backward_rows = lax.psum(padded, ('row', 'col')).astype(jnp.bfloat16)  68.5 us
    psum x1, waiting for transfers between devices, per_device(): scale_grad, bgrad_data = lax.psum((scale_terms, bgrad_terms), ('dp', 'row'))  56.9 us
    dot_general x8, matrix products, contract_product(): lax.dot_general(left, right, (((left_dim,), (right_dim,)), ((), ())), pre...  16.8 us
    dot_general x1, matrix products, per_device(): jnp.dot(portion, frozen_weight, preferred_element_type=jnp.float32)  14.4 us
    psum x1, blocking collectives, per_device(): scale_grad, bgrad_data = lax.psum((scale_terms, bgrad_terms), ('dp', 'row'))  12.1 us
    unnamed x24, local copies, waits for them, and re-layouts  9.11 us
  transfers between devices with their start and end apart: 8, of which 6 were waited for; matrix products, arithmetic and copies ran while one was open for 12% of the time, Pallas kernels for 0%

profile of v1, /device:TPU:0, one launch (start us, length us, event | category | flops | bytes accessed | tf_op | source)
XLA Modules:
  0.0 364.9 jit_solution(3720067078393233731)
XLA Ops:
  7.2 3.1 collective-permute-start
  10.3 25.4 %collective-permute-done = bf16[256,2048]{1,0:T(8,128)(2,1)S(1)} collective-permute-done((bf16[256,2048]{1,0:T(8,128)(2,1)}, bf16[256,2048]{1,0:T(8,128)(2,1)S(1)}, u32[]{:S(2)}, u32[]{:S(2)}) %collective-permute-start) | collective-permute-done | bytes 1048608 | tf_op jit(solution)/shard_map/ppermute | solution.py:45
  35.7 26.1 %collective-permute-done.1 = bf16[256,2048]{1,0:T(8,128)(2,1)S(1)} collective-permute-done((bf16[256,2048]{1,0:T(8,128)(2,1)S(1)}, bf16[256,2048]{1,0:T(8,128)(2,1)S(1)}, u32[]{:S(2)}, u32[]{:S(2)}) %collective-permute-start.1) | collective-permute-done | bytes 1048608 | tf_op jit(solution)/shard_map/ppermute | solution.py:45
  61.9 25.4 %collective-permute-done.2 = bf16[256,2048]{1,0:T(8,128)(2,1)} collective-permute-done((bf16[256,2048]{1,0:T(8,128)(2,1)S(1)}, bf16[256,2048]{1,0:T(8,128)(2,1)}, u32[]{:S(2)}, u32[]{:S(2)}) %collective-permute-start.2) | collective-permute-done | bytes 1048608 | tf_op jit(solution)/shard_map/ppermute | solution.py:45
  87.2 1.3 constant_dynamic-update-slice_fusion.7
  88.7 1.3 constant_dynamic-update-slice_fusion.4
  90.1 1.3 constant_dynamic-update-slice_fusion.3
  91.7 3.2 copy-done.4
  94.9 1.8 fusion
  96.8 14.4 %fusion.2 = f32[1024,2048]{1,0:T(8,128)} fusion(bf16[2048,2048]{1,0:T(8,128)(2,1)} %param.8, bf16[2048,2048]{1,0:T(8,128)(2,1)} %copy-done.4, s32[]{:T(128)S(6)} %select_n.24), kind=kOutput, calls=%fused_computation.3 | convolution fusion | flops 8589934592 | bytes 20971524 | tf_op jit(solution)/shard_map/dot_general | solution.py:49
  111.3 0.1 fusion.21
  111.4 4.6 %fusion.20 = f32[16,2048]{1,0:T(8,128)S(1)} fusion(bf16[16,2048]{1,0:T(8,128)(2,1)S(1)} %copy-done, bf16[2048,2048]{1,0:T(8,128)(2,1)} %param.8), kind=kOutput, calls=%fused_computation.46 | convolution fusion | flops 134217728 | bytes 8585216 | tf_op jit(solution)/shard_map/dot_general | solution.py:38
  116.1 0.9 convolution_add_fusion
  117.0 5.9 %multiply_reduce_fusion = f32[2048]{0:T(1024)S(1)} fusion(bf16[2048,2048]{1,0:T(8,128)(2,1)} %param.8, bf16[16,2048]{1,0:T(8,128)(2,1)S(1)} %copy-done, bf16[16,2048]{1,0:T(8,128)(2,1)S(1)} %copy-done.2), kind=kOutput, calls=%fused_computation | convolution fusion | flops 150992896 | bytes 8527872 | tf_op jit(solution)/shard_map/dot_general | solution.py:11
  122.9 0.2 reduce-window.4
  123.1 5.7 %psum.42 = f32[2048]{0:T(1024)S(1)} all-reduce(f32[2048]{0:T(1024)S(1)} %multiply_reduce_fusion), channel_id=1, replica_groups=mesh['dp'=2,'row'=4,'col'=4] {'row'}, use_global_device_ids=true, to_apply=%region_3.4 | all-reduce | flops 2048 | bytes 16384 | tf_op jit(solution)/shard_map/psum | solution.py:55
  129.0 0.5 convolution_dynamic-update-slice_fusion
  129.5 68.5 %psum.44 = bf16[1024,16]{1,0:T(8,128)(2,1)S(1)} all-reduce(f32[1024,16]{1,0:T(8,128)S(1)} %convolution_dynamic-update-slice_fusion), channel_id=1, replica_groups=mesh['dp'=2,'row'=4,'col'=4] {'row','col'}, use_global_device_ids=true, to_apply=%region_8.9 | all-reduce | flops 16384 | bytes 98304 | tf_op jit(solution)/shard_map/psum | solution.py:85
  198.1 1.8 fusion.5
  199.9 1.2 fusion.14
  201.1 4.1 %multiply_reduce_fusion.1 = (f32[2048]{0:T(1024)}, bf16[256,2048]{1,0:T(8,128)(2,1)}) fusion(bf16[256,2048]{1,0:T(8,128)(2,1)} %param.12, f32[256]{0:T(256)} %copy-done.6, f32[256,2048]{1,0:T(8,128)} %reduce-scatter.3.cloned.1.call-done, f32[256,2048]{1,0:T(8,128)S(1)} %fusion.14, f32[2048]{0:T(1024)S(1)} %fusion.12), kind=kLoop, calls=%fused_computation.10 | loop fusion | flops 3667968 | bytes 6308864 | tf_op jit(solution)/shard_map/reduce_sum | solution.py:71
  205.2 12.1 %psum.43 = f32[2048]{0:T(1024)S(1)} all-reduce(f32[2048]{0:T(1024)} %get-tuple-element.4), channel_id=1, replica_groups=mesh['dp'=2,'row'=4,'col'=4] {'dp','row'}, use_global_device_ids=true, to_apply=%region_7.8 | all-reduce | flops 2048 | bytes 16384 | tf_op jit(solution)/shard_map/psum | solution.py:74
  217.4 1.3 fusion.10
  218.7 5.7 %fusion.7 = f32[16,2048]{1,0:T(8,128)S(1)} fusion(bf16[2048,2048]{1,0:T(8,128)(2,1)} %param.8, bf16[16,2048]{1,0:T(8,128)(2,1)S(1)} %copy-done.2, f32[2048]{0:T(1024)S(1)} %get-tuple-element.6), kind=kOutput, calls=%fused_computation.19 | convolution fusion | flops 134316032 | bytes 8593408 | tf_op jit(solution)/shard_map/dot_general | solution.py:11
  224.3 0.1 fusion.6
  224.5 0.2 fusion.4
  224.7 0.9 convolution_add_fusion.2
  225.7 0.7 all-reduce.8.cloned.1.call-done
  226.3 56.9 %all-reduce.6.cloned.1.call-done = f32[16,2048]{1,0:T(8,128)} async-done(((f32[16,2048]{1,0:T(8,128)}), f32[16,2048]{1,0:T(8,128)}) %all-reduce.6.cloned.1.call-update) | async-done | bytes 131088 | tf_op jit(solution)/shard_map/psum | solution.py:74
  283.3 1.6 multiply_add_fusion
  284.9 71.9 %all-reduce.4.cloned.1.call-done = f32[16,2048]{1,0:T(8,128)} async-done(((f32[16,2048]{1,0:T(8,128)}), f32[16,2048]{1,0:T(8,128)}) %all-reduce.4.cloned.1.call-update) | async-done | bytes 131088 | tf_op jit(solution)/shard_map/psum | solution.py:97
  356.8 1.6 copy.22
  (40 shorter events, 1.0 us)
Async XLA Ops:
  7.2 87.7 %copy-start = (bf16[16,2048]{1,0:T(8,128)(2,1)S(1)}, bf16[16,2048]{1,0:T(8,128)(2,1)}, u32[]{:S(2)}) copy-start(bf16[16,2048]{1,0:T(8,128)(2,1)} %param.9) | copy-start | bytes 196612
  7.2 84.4 %copy-start.1 = (bf16[256,2048]{1,0:T(8,128)(2,1)S(1)}, bf16[256,2048]{1,0:T(8,128)(2,1)}, u32[]{:S(2)}) copy-start(bf16[256,2048]{1,0:T(8,128)(2,1)} %param.7) | copy-start | bytes 3145732
  7.2 190.9 %reduce-scatter.5.cloned.1.call-start = ((), (), s32[]{:S(2)}) async-start(), calls=%async_computation.3 | async-start | bytes 81920 | tf_op jit(solution)/shard_map/reduce_scatter | solution.py:53
  7.2 28.5 %collective-permute-start = (bf16[256,2048]{1,0:T(8,128)(2,1)}, bf16[256,2048]{1,0:T(8,128)(2,1)S(1)}, u32[]{:S(2)}, u32[]{:S(2)}) collective-permute-start(bf16[256,2048]{1,0:T(8,128)(2,1)} %param.7), channel_id=1, source_target_pairs={{0,1},{1,2},{2,3},{3,0},{4,5},{5,6},{6,7},{7,4},{8,9},{9,10},{10,1... | collective-permute-start | bytes 3145736 | tf_op jit(solution)/shard_map/ppermute | solution.py:45
  35.7 26.1 %collective-permute-start.1 = (bf16[256,2048]{1,0:T(8,128)(2,1)S(1)}, bf16[256,2048]{1,0:T(8,128)(2,1)S(1)}, u32[]{:S(2)}, u32[]{:S(2)}) collective-permute-start(bf16[256,2048]{1,0:T(8,128)(2,1)S(1)} %collective-permute-done), channel_id=1, source_target_pairs={{0,1},{1,2},{2,3},{3,0},{4,5},{5,6},{6,7},{7,4},{8,9},{9,10},{10,1... | collective-permute-start | bytes 3145736 | tf_op jit(solution)/shard_map/ppermute | solution.py:45
  61.9 25.4 %collective-permute-start.2 = (bf16[256,2048]{1,0:T(8,128)(2,1)S(1)}, bf16[256,2048]{1,0:T(8,128)(2,1)}, u32[]{:S(2)}, u32[]{:S(2)}) collective-permute-start(bf16[256,2048]{1,0:T(8,128)(2,1)S(1)} %collective-permute-done.1), channel_id=1, source_target_pairs={{0,1},{1,2},{2,3},{3,0},{4,5},{5,6},{6,7},{7,4},{8,9},{9,10},{10,1... | collective-permute-start | bytes 3145736 | tf_op jit(solution)/shard_map/ppermute | solution.py:45
  91.7 3.2 copy-start.4
  96.7 104.4 %reduce-scatter.3.cloned.1.call-start = ((), (), s32[]{:S(2)}) async-start(), calls=%async_computation.2 | async-start | bytes 10485760 | tf_op jit(solution)/shard_map/reduce_scatter | solution.py:52
  111.2 4.8 %copy-start.2 = (bf16[16,2048]{1,0:T(8,128)(2,1)S(1)}, bf16[16,2048]{1,0:T(8,128)(2,1)}, u32[]{:S(2)}) copy-start(bf16[16,2048]{1,0:T(8,128)(2,1)} %param.10) | copy-start | bytes 196612
  111.3 115.1 %all-reduce.8.cloned.1.call-start = ((), (), s32[]{:S(2)}) async-start(), calls=%async_computation.6 | async-start | bytes 262144 | tf_op jit(solution)/shard_map/psum | solution.py:55
  116.9 6.0 %copy-start.7 = (s32[1,8]{1,0:T(1,128)S(1)}, s32[1,8]{1,0:T(1,128)}, u32[]{:S(2)}) copy-start(s32[1,8]{1,0:T(1,128)} %param.13) | copy-start | bytes 100
  116.9 11.9 %copy-start.5 = (f32[2048]{0:T(1024)S(1)}, f32[2048]{0:T(1024)}, u32[]{:S(2)}) copy-start(f32[2048]{0:T(1024)} %param.11) | copy-start | bytes 24580
  117.0 12.1 %copy-start.3 = (bf16[256,2048]{1,0:T(8,128)(2,1)S(1)}, bf16[256,2048]{1,0:T(8,128)(2,1)}, u32[]{:S(2)}) copy-start(bf16[256,2048]{1,0:T(8,128)(2,1)} %param.12) | copy-start | bytes 3145732
  117.0 166.3 %all-reduce.6.cloned.1.call-start = ((), (), s32[]{:S(2)}) async-start(), calls=%async_computation.5 | async-start | bytes 262144 | tf_op jit(solution)/shard_map/psum | solution.py:74
  129.0 70.9 %copy-start.6 = (f32[256]{0:T(256)}, f32[256]{0:T(256)S(1)}, u32[]{:S(2)}) copy-start(f32[256]{0:T(256)S(1)} %select_reduce_fusion) | copy-start | bytes 3076
  199.9 156.9 %all-reduce.4.cloned.1.call-start = ((), (), s32[]{:S(2)}) async-start(), calls=%async_computation.4 | async-start | bytes 262144 | tf_op jit(solution)/shard_map/psum | solution.py:97
Sparse Core Ops, SparseCore 0:
  96.8 17.3 reduce-scatter.4
  116.8 75.6 reduce-scatter.2
  194.8 31.4 all-reduce.7
  229.8 53.4 all-reduce.5
  287.1 69.7 all-reduce.3
